TPU v7x, 32 devices: a whole 2x2x4 slice. The times are simulated.
32 devices in a mesh: space: 16 (over z, y, x), tm: 2 (over core).
Axes of the slice: x: 2, y: 2, z: 4, core: 2. Of those that a mesh axis runs over, the one named last changes fastest.
Arguments:
- vectors: bfloat16 [2, 64, 2, 12, 2048], P('tm', None, None, None, 'space'), may hold values from -6 to 6
- dilution: int32 [64], replicated, may hold values from 0 to 23
- gamma_ids: int32 [16], replicated, may hold values from 1 to 15
Outputs:
- gram: float32 [2, 1024, 128], P(None, 'space')
- loops: float32 [2, 1024, 2], P(None, 'space')
All inputs are finite; a program needn't handle non-finite values.
Results may differ from a plain program's by a relative error of at most 0.0003.
Values sent between devices are 32-bit elements; how exact they have to be, the bound alone decides.
No kernel may reach another device: no remote copies, remote signals or barrier semaphores. Data moves between devices by JAX's collectives and lax.ppermute only.
A program may use at most 64 MiB of HBM per device.

v0:
```python
from functools import partial
import math

import jax
import jax.numpy as jnp
from jax import lax
from jax.sharding import PartitionSpec as P

TDIL = 2


highest = lax.Precision.HIGHEST


def zero_square():
    return [[0, 0, 0, 0] for _ in range(4)]


def pair_product(left, right):
    real_out = zero_square()
    imag_out = zero_square()
    for row in range(4):
        for col in range(4):
            acc_real = 0
            acc_imag = 0
            for mid in range(4):
                acc_real += (
                    left[0][row][mid] * right[0][mid][col] - left[1][row][mid] * right[1][mid][col]
                )
                acc_imag += (
                    left[0][row][mid] * right[1][mid][col] + left[1][row][mid] * right[0][mid][col]
                )
            real_out[row][col] = acc_real
            imag_out[row][col] = acc_imag
    return (real_out, imag_out)


def dirac_tables():
    factors = [
        (zero_square(), [[0, 0, 0, 1], [0, 0, 1, 0], [0, -1, 0, 0], [-1, 0, 0, 0]]),
        ([[0, 0, 0, -1], [0, 0, 1, 0], [0, 1, 0, 0], [-1, 0, 0, 0]], zero_square()),
        (zero_square(), [[0, 0, 1, 0], [0, 0, 0, -1], [-1, 0, 0, 0], [0, 1, 0, 0]]),
        ([[0, 0, 1, 0], [0, 0, 0, 1], [1, 0, 0, 0], [0, 1, 0, 0]], zero_square()),
    ]
    reals = []
    imags = []
    for number in range(16):
        current = ([[1 if a == b else 0 for b in range(4)] for a in range(4)], zero_square())
        for position in range(4):
            if number >> position & 1:
                current = pair_product(current, factors[position])
        reals.append([value for line in current[0] for value in line])
        imags.append([value for line in current[1] for value in line])
    return (reals, imags)


def pick_gammas(gamma_ids):
    table_real, table_imag = dirac_tables()
    choose = (gamma_ids[:, None] == jnp.arange(16, dtype=jnp.int32)[None, :]).astype(jnp.float32)
    gamma_real = jnp.dot(
        choose, jnp.asarray(table_real, dtype=jnp.float32), precision=highest
    ).reshape(-1, 4, 4)
    gamma_imag = jnp.dot(
        choose, jnp.asarray(table_imag, dtype=jnp.float32), precision=highest
    ).reshape(-1, 4, 4)
    return (gamma_real, gamma_imag)


def shards(vectors, dilution, gamma_ids):
    slices, count, halves, comps, sites = vectors.shape
    owners = lax.axis_size("space")
    total_sites = sites * owners
    gram_scale = 1.0 / math.sqrt(48.0 * total_sites)
    loop_scale = 1.0 / math.sqrt(1.0 * total_sites)
    gamma_real, gamma_imag = pick_gammas(gamma_ids)
    spin_pick = ((dilution % 12 // 3)[:, None] == jnp.arange(4, dtype=jnp.int32)[None, :]).astype(
        jnp.float32
    )
    colour_pick = ((dilution % 3)[:, None] == jnp.arange(3, dtype=jnp.int32)[None, :]).astype(
        jnp.float32
    )
    time_class = dilution // 12
    ein = partial(jnp.einsum, precision=highest)
    lowein = partial(jnp.einsum, preferred_element_type=jnp.float32)
    first_slice = lax.axis_index("tm") * slices
    rows_real = ein("gba,ib->gia", gamma_real, spin_pick)
    rows_imag = ein("gba,ib->gia", gamma_imag, spin_pick)

    def one_slice(inputs):
        block, slice_index = inputs
        spinor = block.reshape(count, 2, 4, 3 * sites)
        real_part = spinor[:, 0]
        imag_part = spinor[:, 1]
        pair_real = lowein("iak,jbk->iajb", real_part, real_part) + lowein(
            "iak,jbk->iajb", imag_part, imag_part
        )
        pair_imag = lowein("iak,jbk->iajb", real_part, imag_part) - lowein(
            "iak,jbk->iajb", imag_part, real_part
        )
        gram_real = ein("gab,iajb->gij", gamma_real, pair_real) - ein(
            "gab,iajb->gij", gamma_imag, pair_imag
        )
        gram_imag = ein("gab,iajb->gij", gamma_real, pair_imag) + ein(
            "gab,iajb->gij", gamma_imag, pair_real
        )
        gram = jnp.concatenate([gram_real, gram_imag], axis=2).reshape(-1, 2 * count)
        gram = gram * gram_scale
        site_sums = jnp.sum(block, axis=-1, dtype=jnp.float32).reshape(count, 2, 4, 3)
        picked = ein("ipac,ic->ipa", site_sums, colour_pick)
        loop_real = ein("gia,ia->gi", rows_real, picked[:, 0]) - ein(
            "gia,ia->gi", rows_imag, picked[:, 1]
        )
        loop_imag = ein("gia,ia->gi", rows_real, picked[:, 1]) + ein(
            "gia,ia->gi", rows_imag, picked[:, 0]
        )
        live = (time_class == slice_index % TDIL).astype(jnp.float32)[None, :]
        loops = jnp.stack([loop_real * live, loop_imag * live], axis=-1).reshape(-1, 2) * loop_scale
        return (gram, loops)

    gram_terms, loop_terms = lax.map(
        one_slice, (vectors, first_slice + jnp.arange(slices, dtype=jnp.int32))
    )
    total_rows = gram_terms.shape[1]
    owned = total_rows // owners
    totals = lax.psum((gram_terms, loop_terms), "space")
    start = lax.axis_index("space") * owned
    shares = (
        lax.dynamic_slice_in_dim(totals[0], start, owned, 1),
        lax.dynamic_slice_in_dim(totals[1], start, owned, 1),
    )
    gram, loops = (
        lax.all_gather(shares[0], "tm", axis=0, tiled=True),
        lax.all_gather(shares[1], "tm", axis=0, tiled=True),
    )
    return (gram, loops)


def solution(mesh):
    placed = (P("tm", None, None, None, "space"), P(), P())
    return jax.shard_map(
        shards,
        mesh=mesh,
        in_specs=placed,
        out_specs=(P(None, "space", None), P(None, "space", None)),
        check_vma=False,
    )
```

profile of v0, /device:TPU:0, one launch (start us, length us, event | category | flops | bytes accessed | tf_op | source)
XLA Modules:
  0.0 139.6 jit_solution(7025486430821576834)
XLA Ops:
  7.2 0.0 all-reduce.2.cloned.1.call-start
  7.2 1.1 copy.30
  8.3 0.3 reshape.78
  8.6 0.1 fusion.36
  8.7 0.3 fusion.10
  9.0 0.3 fusion.8
  9.4 0.0 copy-start.1
  9.4 0.0 copy-start.3
  9.4 0.3 convolution_add_fusion
  9.7 0.3 copy-done.1
  10.0 0.1 copy-done.3
  10.1 0.0 copy-start.4
  10.1 0.2 fusion.27
  10.3 0.5 copy-done.4
  10.8 0.2 fusion.28
  11.0 0.3 convolution_subtract_fusion
  11.3 1.1 convolution_bitcast_fusion
  12.4 1.1 convolution_bitcast_fusion.2
  13.5 1.1 fusion.1
  14.6 1.1 fusion
  15.7 0.2 maximum_multiply_fusion
  15.9 1.0 copy.38
  16.9 0.0 copy-start
  16.9 0.0 all-reduce.2.cloned.1.call-update
  16.9 1.0 copy-done
  17.9 0.9 convert_reduce_fusion
  18.8 0.2 copy.39
  19.0 0.0 copy-start.2
  19.0 0.2 copy.50
  19.2 0.5 copy-done.2
  19.7 0.1 fusion.24
  19.8 0.4 fusion.22
  20.2 0.1 fusion.37
  20.3 0.1 copy.79
  20.3 0.1 copy.80
  20.4 0.2 convolution_bitcast_fusion.4
  20.7 0.2 multiply_reduce_fusion.3
  20.9 0.1 stack.13
  21.0 0.1 stack.12
  21.1 44.1 %psum.15 = f32[1,1024,2]{1,2,0:T(2,128)S(1)} all-reduce(f32[1,1024,2]{1,2,0:T(2,128)S(1)} %maximum_multiply_fusion.1), channel_id=1, replica_groups=mesh['space'=16,'tm'=2] {'space'}, use_global_device_ids=true, to_apply=%region_2.3 | all-reduce | flops 2048 | bytes 16384 | tf_op jit(solution)/shard_map/psum | solution.py:125
  65.2 0.1 constant_dynamic-slice_fusion
  65.3 1.8 %all_gather.7 = f32[2,64,2]{1,2,0:T(2,128)S(1)} all-gather(f32[1,64,2]{1,2,0:T(2,128)S(1)} %constant_dynamic-slice_fusion), channel_id=1, replica_groups=mesh['space'=16,'tm'=2] {'tm'}, dimensions={0}, use_global_device_ids=true | all-gather | bytes 1536 | tf_op jit(solution)/shard_map/all_gather | solution.py:133
  67.1 61.8 %all-reduce.2.cloned.1.call-done = f32[1,1024,128]{2,1,0:T(8,128)} async-done(((f32[1,1024,128]{2,1,0:T(8,128)}), f32[1,1024,128]{2,1,0:T(8,128)}) %all-reduce.2.cloned.1.call-update) | async-done | bytes 524304 | tf_op jit(solution)/shard_map/psum | solution.py:125
  128.9 0.8 constant_dynamic-slice_fusion.1
  129.7 1.8 %all_gather.6 = f32[2,64,128]{2,1,0:T(8,128)S(1)} all-gather(f32[1,64,128]{2,1,0:T(8,128)S(1)} %constant_dynamic-slice_fusion.1), channel_id=1, replica_groups=mesh['space'=16,'tm'=2] {'tm'}, dimensions={0}, use_global_device_ids=true | all-gather | bytes 98304 | tf_op jit(solution)/shard_map/all_gather | solution.py:132
  131.5 0.6 copy.131
  132.1 0.6 copy.132
  (4 shorter events, 0.1 us)
Async XLA Ops:
  7.2 121.7 %all-reduce.2.cloned.1.call-start = ((), (), s32[]{:S(2)}) async-start(), calls=%async_computation | async-start | bytes 1048576 | tf_op jit(solution)/shard_map/psum | solution.py:125
  9.4 0.7 copy-start.1
  9.4 0.7 copy-start.3
  10.1 0.7 copy-start.4
  16.9 1.0 copy-start
  19.0 0.7 copy-start.2
Sparse Core Ops, SparseCore 0:
  17.1 111.7 all-reduce.1
where the time goes:
time: 140 us
  waiting for transfers between devices  61.9 us (44%)
  blocking collectives  47.7 us (34%)
  between operations  14.2 us (10%)
  local copies, waits for them, and re-layouts  7.6 us (5%)
  matrix products  6.88 us (5%)
    psum x1, waiting for transfers between devices, shards(): totals = lax.psum((gram_terms, loop_terms), 'space')  61.8 us
    psum x1, blocking collectives, shards(): totals = lax.psum((gram_terms, loop_terms), 'space')  44.1 us
    unnamed x15, local copies, waits for them, and re-layouts  4.74 us
  transfers between devices with their start and end apart: 1, of which 1 were waited for; matrix products, arithmetic and copies ran while one was open for 2% of the time, Pallas kernels for 0%

commit v1 on v0

--- a/solution.py
+++ b/solution.py
@@ -4,9 +4,16 @@
 import jax
 import jax.numpy as jnp
 from jax import lax
+from jax.experimental import pallas as pl
+from jax.experimental.pallas import tpu as pltpu
 from jax.sharding import PartitionSpec as P
 
 TDIL = 2
+SPINS = 4
+COLOURS = 3
+LANES = 128
+
+EXCHANGE_ORDER = (9, 8, 0, 10, 15, 4, 1, 7, 5, 2, 11, 12, 6, 3, 13, 14)
 
 
 highest = lax.Precision.HIGHEST
@@ -35,27 +42,56 @@
     return (real_out, imag_out)
 
 
-def dirac_tables():
+def dirac_squares():
     factors = [
         (zero_square(), [[0, 0, 0, 1], [0, 0, 1, 0], [0, -1, 0, 0], [-1, 0, 0, 0]]),
         ([[0, 0, 0, -1], [0, 0, 1, 0], [0, 1, 0, 0], [-1, 0, 0, 0]], zero_square()),
         (zero_square(), [[0, 0, 1, 0], [0, 0, 0, -1], [-1, 0, 0, 0], [0, 1, 0, 0]]),
         ([[0, 0, 1, 0], [0, 0, 0, 1], [1, 0, 0, 0], [0, 1, 0, 0]], zero_square()),
     ]
-    reals = []
-    imags = []
+    squares = []
     for number in range(16):
         current = ([[1 if a == b else 0 for b in range(4)] for a in range(4)], zero_square())
         for position in range(4):
             if number >> position & 1:
                 current = pair_product(current, factors[position])
-        reals.append([value for line in current[0] for value in line])
-        imags.append([value for line in current[1] for value in line])
-    return (reals, imags)
+        squares.append(current)
+    return squares
+
+
+def dirac_bits():
+    imaginary, anti, mask_low, mask_high = 0, 0, 0, 0
+    negative = [0, 0, 0, 0]
+    for number, (real, imag) in enumerate(dirac_squares()):
+        places = [[b for b in range(4) if real[a][b] or imag[a][b]] for a in range(4)]
+        mask = places[0][0]
+        assert all(places[a] == [a ^ mask] for a in range(4))
+        kind = int(imag[0][mask] != 0)
+        values = [(imag if kind else real)[a][a ^ mask] for a in range(4)]
+        assert all(abs(v) == 1 for v in values)
+        sign = -1 if kind else 1
+        flips = {values[a] * values[a ^ mask] * sign for a in range(4)}
+        assert len(flips) == 1
+        imaginary |= kind << number
+        anti |= int(flips == {-1}) << number
+        mask_low |= (mask & 1) << number
+        mask_high |= (mask >> 1) << number
+        for a in range(4):
+            negative[a] |= int(values[a] < 0) << number
+    return imaginary, anti, mask_low, mask_high, negative
+
+
+IMAGINARY, ANTI, MASK_LOW, MASK_HIGH, NEGATIVE = dirac_bits()
+
+
+def bit(word, number):
+    return (jnp.int32(word) >> number) & 1
 
 
 def pick_gammas(gamma_ids):
-    table_real, table_imag = dirac_tables()
+    squares = dirac_squares()
+    table_real = [[v for line in real for v in line] for real, _ in squares]
+    table_imag = [[v for line in imag for v in line] for _, imag in squares]
     choose = (gamma_ids[:, None] == jnp.arange(16, dtype=jnp.int32)[None, :]).astype(jnp.float32)
     gamma_real = jnp.dot(
         choose, jnp.asarray(table_real, dtype=jnp.float32), precision=highest
@@ -66,7 +102,198 @@
     return (gamma_real, gamma_imag)
 
 
-def shards(vectors, dilution, gamma_ids):
+def half_swap(value, count):
+    return pltpu.roll(value, count, 1)
+
+
+def partial_kernel(
+    count, order, ids_ref, dilution_ref, block_ref, out_ref, flat_ref, left_ref, right_ref, pair_ref, loop_ref
+):
+    comps = SPINS * COLOURS
+    width = COLOURS * LANES
+    rows = count // 2
+    flat_ref[...] = block_ref[...].astype(jnp.float32)
+    for spin in range(SPINS):
+        for part in range(2):
+            for colour in range(COLOURS):
+                start = (spin * COLOURS + colour) * 2 + part
+                piece = flat_ref[pl.ds(start, count, stride=2 * comps), :]
+                here = pl.ds(spin * count, count)
+                lanes = pl.ds(part * width + colour * LANES, LANES)
+                other = pl.ds((1 - part) * width + colour * LANES, LANES)
+                left_ref[here, lanes] = piece.astype(jnp.bfloat16)
+                right_ref[here, other] = (piece if part else -piece).astype(jnp.bfloat16)
+    total = SPINS * count
+    row_id = lax.broadcasted_iota(jnp.int32, (16, 2 * width), 0)
+    lane_id = lax.broadcasted_iota(jnp.int32, (16, 2 * width), 1)
+    ones = jnp.where(lane_id // LANES == row_id, 1.0, 0.0) * jnp.where(row_id < COLOURS, 1.0, 0.0)
+    left_ref[pl.ds(total, 16), :] = ones.astype(jnp.bfloat16)
+    dims = (((1,), (1,)), ((), ()))
+    real = lax.dot_general(
+        left_ref[...], left_ref[pl.ds(0, total), :], dims, preferred_element_type=jnp.float32
+    )
+    imag = lax.dot_general(left_ref[...], right_ref[...], dims, preferred_element_type=jnp.float32)
+    columns = total // LANES
+    for spin in range(SPINS):
+        for column in range(columns):
+            r = real[spin * count : (spin + 1) * count, column * LANES : (column + 1) * LANES]
+            i = imag[spin * count : (spin + 1) * count, column * LANES : (column + 1) * LANES]
+            pair_ref[0, spin, column] = r + i
+            pair_ref[1, spin, column] = r - i
+
+    lane = lax.broadcasted_iota(jnp.int32, (1, LANES), 1)
+    high = lane >= count
+    half = high.astype(jnp.int32)
+    index = jnp.concatenate([dilution_ref[...]] * 2, axis=1)
+    spin_of = index % comps // COLOURS
+    colour_of = index % COLOURS
+    sums = []
+    for grid in (real, imag):
+        for column in range(columns):
+            picked = jnp.zeros((1, LANES), jnp.float32)
+            for colour in range(COLOURS):
+                row = grid[total + colour : total + colour + 1, column * LANES : (column + 1) * LANES]
+                picked = jnp.where(colour_of == colour, row, picked)
+            sums.append(picked)
+    for mask in range(4):
+        source = spin_of ^ mask
+        found = []
+        for part in range(2):
+            lower, upper = sums[part * columns], sums[part * columns + 1]
+            value = jnp.where(source >= 2, upper, lower)
+            value = jnp.where((source & 1) == half, value, 0.0)
+            found.append(value + half_swap(value, count))
+        loop_ref[0, mask] = jnp.where(high, found[1], found[0])
+        loop_ref[1, mask] = jnp.where(high, found[0], -found[1])
+
+    wide_high = lax.broadcasted_iota(jnp.int32, (rows, LANES), 1) >= count
+    for place, owner in enumerate(order):
+        number = ids_ref[owner]
+        imaginary, anti = bit(IMAGINARY, number), bit(ANTI, number)
+        low, upper = bit(MASK_LOW, number), bit(MASK_HIGH, number)
+        signs = [1 - 2 * bit(NEGATIVE[a], number) for a in range(4)]
+        turn = 1 - 2 * (anti & (1 - imaginary))
+        kind = imaginary ^ anti
+        odd = wide_high.astype(jnp.int32) == low
+        halves = []
+        for top in range(2):
+            here = pl.ds(top * rows, rows)
+            gathered = None
+            for pair in range(2):
+                column = upper ^ pair
+                even_sign = (signs[2 * pair] * turn).astype(jnp.float32)
+                odd_sign = (signs[2 * pair + 1] * turn).astype(jnp.float32)
+                term = jnp.where(
+                    odd,
+                    even_sign * pair_ref[kind, 2 * pair, column, here, :],
+                    odd_sign * pair_ref[kind, 2 * pair + 1, column, here, :],
+                )
+                gathered = term if gathered is None else gathered + term
+            halves.append(gathered)
+        kept = jnp.where(wide_high, halves[1], halves[0])
+        moved = jnp.where(wide_high, halves[0], halves[1])
+        base = place * (rows + 1)
+        out_ref[pl.ds(base, rows), :] = kept + half_swap(moved, count)
+        sign = jnp.zeros((1, LANES), jnp.int32)
+        for a in range(4):
+            sign = jnp.where(spin_of == a, signs[a], sign)
+        mask = low + 2 * upper
+        out_ref[pl.ds(base + rows, 1), :] = sign.astype(jnp.float32) * loop_ref[imaginary, mask]
+
+
+def sum_kernel(chunks, rows, parts_ref, out_ref):
+    total = parts_ref[pl.ds(0, rows), :]
+    for chunk in range(1, chunks):
+        total = total + parts_ref[pl.ds(chunk * rows, rows), :]
+    out_ref[...] = total
+
+
+def finish_kernel(count, gram_scale, loop_scale, ids_ref, dilution_ref, mine_ref, other_ref, gram_ref, loop_ref):
+    rows = count // 2
+    own = lax.axis_index("tm")
+    number = ids_ref[lax.axis_index("space")]
+    anti = bit(ANTI, number)
+    high = lax.broadcasted_iota(jnp.int32, (rows, LANES), 1) >= count
+    full_high = lax.broadcasted_iota(jnp.int32, (count, LANES), 1) >= count
+    time_class = dilution_ref[...] // (SPINS * COLOURS)
+    for ref, slice_index in ((mine_ref, own), (other_ref, 1 - own)):
+        packed = ref[pl.ds(0, rows), :]
+        swapped = half_swap(packed, count)
+        square = jnp.concatenate(
+            [jnp.where(high, swapped, packed), jnp.where(high, packed, swapped)], axis=0
+        )
+        turned = jnp.transpose(jnp.concatenate([square, square], axis=0))[:count]
+        real = (square + turned) * (0.5 * gram_scale)
+        imag = (square - turned) * (0.5 * gram_scale)
+        plain = jnp.where(full_high, imag, real)
+        rotated = jnp.where(full_high, real, -imag)
+        gram_ref[slice_index] = jnp.where(anti == 1, rotated, plain)
+        row = ref[pl.ds(rows, 1), :] * loop_scale
+        both = jnp.concatenate([row, half_swap(row, count)], axis=0)
+        live = (time_class == slice_index % TDIL).astype(jnp.float32)
+        loop_ref[slice_index] = both[:, :count] * live
+
+
+def packed_shards(vectors, dilution, gamma_ids):
+    slices, count, halves, comps, sites = vectors.shape
+    owners = lax.axis_size("space")
+    total_sites = sites * owners
+    gram_scale = 1.0 / math.sqrt(48.0 * total_sites)
+    loop_scale = 1.0 / math.sqrt(1.0 * total_sites)
+    order = EXCHANGE_ORDER if owners == len(EXCHANGE_ORDER) else tuple(range(owners))
+    rows = count // 2
+    chunk = rows + 1
+    block = jnp.transpose(vectors, (0, 1, 3, 2, 4)).reshape(count * comps * halves, sites)
+    vmem = pl.BlockSpec(memory_space=pltpu.VMEM)
+    smem = pl.BlockSpec(memory_space=pltpu.SMEM)
+    total = SPINS * count
+    parts = pl.pallas_call(
+        partial(partial_kernel, count, order),
+        out_shape=jax.ShapeDtypeStruct((owners * chunk, LANES), jnp.float32),
+        in_specs=[smem, vmem, vmem],
+        out_specs=vmem,
+        scratch_shapes=[
+            pltpu.VMEM((count * comps * halves, LANES), jnp.float32),
+            pltpu.VMEM((total + 16, 2 * COLOURS * LANES), jnp.bfloat16),
+            pltpu.VMEM((total, 2 * COLOURS * LANES), jnp.bfloat16),
+            pltpu.VMEM((2, SPINS, total // LANES, count, LANES), jnp.float32),
+            pltpu.VMEM((2, 4, 1, LANES), jnp.float32),
+        ],
+        compiler_params=pltpu.CompilerParams(vmem_limit_bytes=16 << 20),
+        name="partial_gram",
+    )(gamma_ids, dilution.reshape(1, count), block)
+    swapped = lax.all_to_all(
+        parts.reshape(owners, chunk, 1, LANES),
+        "space",
+        0,
+        0,
+        tiled=True,
+        axis_index_groups=[list(order)],
+    )
+    mine = pl.pallas_call(
+        partial(sum_kernel, owners, chunk),
+        out_shape=jax.ShapeDtypeStruct((chunk, LANES), jnp.float32),
+        in_specs=[vmem],
+        out_specs=vmem,
+        compiler_params=pltpu.CompilerParams(vmem_limit_bytes=4 << 20),
+        name="sum_chunks",
+    )(swapped.reshape(owners * chunk, LANES))
+    other = lax.ppermute(mine, "tm", [(0, 1), (1, 0)])
+    gram, loops = pl.pallas_call(
+        partial(finish_kernel, count, gram_scale, loop_scale),
+        out_shape=(
+            jax.ShapeDtypeStruct((2, count, LANES), jnp.float32),
+            jax.ShapeDtypeStruct((2, 2, count), jnp.float32),
+        ),
+        in_specs=[smem, vmem, vmem, vmem],
+        out_specs=(vmem, vmem),
+        compiler_params=pltpu.CompilerParams(vmem_limit_bytes=4 << 20),
+        name="finish",
+    )(gamma_ids, dilution.reshape(1, count), mine, other)
+    return gram, jnp.transpose(loops, (0, 2, 1))
+
+
+def general_shards(vectors, dilution, gamma_ids):
     slices, count, halves, comps, sites = vectors.shape
     owners = lax.axis_size("space")
     total_sites = sites * owners
@@ -120,23 +347,33 @@
     gram_terms, loop_terms = lax.map(
         one_slice, (vectors, first_slice + jnp.arange(slices, dtype=jnp.int32))
     )
-    total_rows = gram_terms.shape[1]
-    owned = total_rows // owners
-    totals = lax.psum((gram_terms, loop_terms), "space")
-    start = lax.axis_index("space") * owned
-    shares = (
-        lax.dynamic_slice_in_dim(totals[0], start, owned, 1),
-        lax.dynamic_slice_in_dim(totals[1], start, owned, 1),
-    )
-    gram, loops = (
-        lax.all_gather(shares[0], "tm", axis=0, tiled=True),
-        lax.all_gather(shares[1], "tm", axis=0, tiled=True),
-    )
-    return (gram, loops)
+    owned = gram_terms.shape[1] // owners
+    width = 2 * count
+    padded = jnp.pad(loop_terms, ((0, 0), (0, 0), (0, width - 2)))
+    terms = jnp.stack([gram_terms, padded], axis=1).reshape(slices * 2, owners, owned, width)
+    swapped = lax.all_to_all(terms, "space", 1, 1, tiled=True)
+    mine = jnp.sum(swapped, axis=1).reshape(slices, 2, owned, width)
+    every = lax.all_gather(mine, "tm", axis=0, tiled=True)
+    return (every[:, 0], every[:, 1, :, :2])
 
 
 def solution(mesh):
     placed = (P("tm", None, None, None, "space"), P(), P())
+
+    def shards(vectors, dilution, gamma_ids):
+        slices, count, halves, comps, sites = vectors.shape
+        packable = (
+            slices == 1
+            and mesh.shape["tm"] == 2
+            and gamma_ids.shape[0] == mesh.shape["space"]
+            and 2 * count == LANES
+            and comps == SPINS * COLOURS
+            and halves == 2
+            and sites == LANES
+        )
+        body = packed_shards if packable else general_shards
+        return body(vectors, dilution, gamma_ids)
+
     return jax.shard_map(
         shards,
         mesh=mesh,

time: 140 us -> 22.5 us (0.16)
  waiting for transfers between devices: 61.9 us -> 1.18 us
  blocking collectives: 47.7 us -> 16 us
  between operations: 14.2 us -> 0.66 us
  matrix products: 6.88 us -> 0 us
  local copies, waits for them, and re-layouts: 7.6 us -> 1.65 us
  Pallas kernels: 0 us -> 2.74 us
    psum x1 -> x0, waiting for transfers between devices: 61.8 us -> none  [shards(): totals = lax.psum((gram_terms, loop_terms), 'space')]
    psum x1 -> x0, blocking collectives: 44.1 us -> none  [shards(): totals = lax.psum((gram_terms, loop_terms), 'space')]
    all_to_all x0 -> x1, blocking collectives: none -> 16 us  [packed_shards(): lax.all_to_all(parts.reshape(owners, chunk, 1, LANES), 'space', 0, 0, til...]
    dot_general x13 -> x0, matrix products: 6.88 us -> none  [the longest x1 1.09 us: one_slice(): ein('gab,iajb->gij', gamma_imag, pair_real)]
    all_gather x2 -> x0, blocking collectives: 3.64 us -> none  [the longest x1 1.84 us: shards(): lax.all_gather(shares[0], 'tm', axis=0, tiled=True)]
    unnamed x15 -> x6, local copies, waits for them, and re-layouts: 4.74 us -> 1.65 us
    pallas_call x0 -> x3, Pallas kernels: none -> 2.74 us  [the longest x1 1.38 us: packed_shards(): pl.pallas_call(partial(partial_kernel, count, order), out_shape=jax.Shape...]
  transfers between devices with their start and end apart: 1 -> 1, of which waited for: 1 -> 1; matrix products, arithmetic and copies ran while one was open for 2% -> 0% of each run, Pallas kernels for 0% -> 0%
where the time goes in v1:
time: 22.5 us; the launch traced here: 22.3 us
  blocking collectives  16 us (71%)
  Pallas kernels  2.74 us (12%)
  local copies, waits for them, and re-layouts  1.65 us (7%)
  waiting for transfers between devices  1.18 us (5%)
  between operations  0.66 us (3%)
    all_to_all x1, blocking collectives, packed_shards(): lax.all_to_all(parts.reshape(owners, chunk, 1, LANES), 'space', 0, 0, til...  16 us
    unnamed x6, local copies, waits for them, and re-layouts  1.65 us
    pallas_call x1, Pallas kernels, packed_shards(): pl.pallas_call(partial(partial_kernel, count, order), out_shape=jax.Shape...  1.38 us
    pallas_call x1, Pallas kernels, packed_shards(): pl.pallas_call(partial(finish_kernel, count, gram_scale, loop_scale), out...  1.33 us
    ppermute x1, waiting for transfers between devices, packed_shards(): other = lax.ppermute(mine, 'tm', [(0, 1), (1, 0)])  1.18 us
  transfers between devices with their start and end apart: 1, of which 1 were waited for; matrix products, arithmetic and copies ran while one was open for 0% of the time, Pallas kernels for 0%

profile of v1, /device:TPU:0, one launch (start us, length us, event | category | flops | bytes accessed | tf_op | source)
XLA Modules:
  0.0 22.3 jit_solution(17185529758786169747)
XLA Ops:
  0.6 0.0 copy-start.1
  0.6 0.0 copy-start.2
  0.6 0.6 %copy-done.1 = s32[16]{0:T(128)S(1)} copy-done((s32[16]{0:T(128)S(1)}, s32[16]{0:T(128)}, u32[]{:S(2)}) %copy-start.1) | copy-done | bytes 88
  1.3 0.0 copy-done.2
  1.3 0.0 copy-start
  1.3 1.0 %copy-done = bf16[1,64,2,12,128]{4,2,3,1,0:T(2,128)(2,1)S(1)} copy-done((bf16[1,64,2,12,128]{4,2,3,1,0:T(2,128)(2,1)S(1)}, bf16[1,64,2,12,128]{4,2,3,1,0:T(2,128)(2,1)}, u32[]{:S(2)}) %copy-start) | copy-done | bytes 393240
  2.3 1.4 %partial_gram.1 = f32[528,128]{1,0:T(8,128)S(1)} custom-call(s32[16]{0:T(128)S(1)} %copy-done.1, s32[1,64]{1,0:T(1,128)S(1)} %bitcast.10, bf16[1536,128]{1,0:T(8,128)(2,1)S(1)} %bitcast.9), custom_call_target="tpu_custom_call" | custom-call | tf_op jit(solution)/shard_map/partial_gram/pallas_call | solution.py:250
  3.7 16.0 %all_to_all.5 = f32[16,33,1,128]{3,2,1,0:T(1,128)S(1)} all-to-all(f32[16,33,1,128]{3,2,1,0:T(1,128)S(1)} %bitcast.8), channel_id=1, replica_groups={{18,16,0,20,30,8,2,14,10,4,22,24,12,6,26,28},{19,17,1,21,31,9,3,15,11,5..., dimensions={0} | all-to-all | bytes 540672 | tf_op jit(solution)/shard_map/all_to_all | solution.py:265
  19.7 0.1 collective-permute-start
  19.8 1.2 %collective-permute-done.other_ref = f32[33,128]{1,0:T(8,128)S(1)} collective-permute-done((f32[33,128]{1,0:T(8,128)S(1)}, f32[33,128]{1,0:T(8,128)S(1)}, u32[]{:S(2)}, u32[]{:S(2)}) %collective-permute-start) | collective-permute-done | bytes 16928 | tf_op jit(solution)/shard_map/ppermute | solution.py:281
  21.0 1.3 %finish.1 = (f32[2,64,128]{2,1,0:T(8,128)}, f32[2,2,64]{2,1,0:T(2,128)}) custom-call(s32[16]{0:T(128)S(1)} %copy-done.1, s32[1,64]{1,0:T(1,128)S(1)} %bitcast.11, f32[33,128]{1,0:T(8,128)S(1)} %sum_chunks.1.mine_ref, f32[33,128]{1,0:T(8,128)S(1)} %collective-permute-done.other_ref), custom_call_target="tpu_custom_call" | custom-call | tf_op jit(solution)/shard_map/finish/pallas_call | solution.py:282
  (1 shorter events, 0.0 us)
Async XLA Ops:
  0.6 0.7 %copy-start.1 = (s32[16]{0:T(128)S(1)}, s32[16]{0:T(128)}, u32[]{:S(2)}) copy-start(s32[16]{0:T(128)} %ids_ref.3) | copy-start | bytes 196
  0.6 0.7 %copy-start.2 = (s32[64]{0:T(128)S(1)}, s32[64]{0:T(128)}, u32[]{:S(2)}) copy-start(s32[64]{0:T(128)} %param.4) | copy-start | bytes 772
  1.3 1.0 %copy-start = (bf16[1,64,2,12,128]{4,2,3,1,0:T(2,128)(2,1)S(1)}, bf16[1,64,2,12,128]{4,2,3,1,0:T(2,128)(2,1)}, u32[]{:S(2)}) copy-start(bf16[1,64,2,12,128]{4,2,3,1,0:T(2,128)(2,1)} %param.3) | copy-start | bytes 1179652
  19.7 1.3 %collective-permute-start = (f32[33,128]{1,0:T(8,128)S(1)}, f32[33,128]{1,0:T(8,128)S(1)}, u32[]{:S(2)}, u32[]{:S(2)}) collective-permute-start(f32[33,128]{1,0:T(8,128)S(1)} %sum_chunks.1.mine_ref), channel_id=1, source_target_pairs={{0,1},{1,0},{2,3},{3,2},{4,5},{5,4},{6,7},{7,6},{8,9},{9,8},{10,11... | collective-permute-start | bytes 50696 | tf_op jit(solution)/shard_map/ppermute | solution.py:281

commit v2 on v1

--- a/solution.py
+++ b/solution.py
@@ -12,8 +12,9 @@
 SPINS = 4
 COLOURS = 3
 LANES = 128
-
-EXCHANGE_ORDER = (9, 8, 0, 10, 15, 4, 1, 7, 5, 2, 11, 12, 6, 3, 13, 14)
+PIECES = 4
+
+EXCHANGE_ORDER = (8, 1, 7, 10, 14, 15, 13, 4, 9, 11, 5, 2, 12, 0, 6, 3)
 
 
 highest = lax.Precision.HIGHEST
@@ -102,45 +103,86 @@
     return (gamma_real, gamma_imag)
 
 
+def in_hbm(value):
+    return pltpu.with_memory_space_constraint(value, pltpu.HBM)
+
+
 def half_swap(value, count):
     return pltpu.roll(value, count, 1)
 
 
 def partial_kernel(
-    count, order, ids_ref, dilution_ref, block_ref, out_ref, flat_ref, left_ref, right_ref, pair_ref, loop_ref
+    count, order, loop_scale, ids_hbm, dilution_hbm, block_hbm, out_ref, notes_ref,
+    ids_ref, dilution_ref, block_ref, flat_ref, left_ref, right_ref, kept_ref, loop_ref, sems,
 ):
     comps = SPINS * COLOURS
     width = COLOURS * LANES
     rows = count // 2
-    flat_ref[...] = block_ref[...].astype(jnp.float32)
-    for spin in range(SPINS):
-        for part in range(2):
-            for colour in range(COLOURS):
-                start = (spin * COLOURS + colour) * 2 + part
-                piece = flat_ref[pl.ds(start, count, stride=2 * comps), :]
-                here = pl.ds(spin * count, count)
-                lanes = pl.ds(part * width + colour * LANES, LANES)
-                other = pl.ds((1 - part) * width + colour * LANES, LANES)
-                left_ref[here, lanes] = piece.astype(jnp.bfloat16)
-                right_ref[here, other] = (piece if part else -piece).astype(jnp.bfloat16)
     total = SPINS * count
+    columns = total // LANES
+    pieces = PIECES
+    batch = count // pieces
+    span = batch * comps * 2
+    copies = [
+        pltpu.make_async_copy(
+            block_hbm.at[pl.ds(piece * span, span), :],
+            block_ref.at[pl.ds(piece * span, span), :],
+            sems.at[piece],
+        )
+        for piece in range(pieces)
+    ]
+    for copy in copies:
+        copy.start()
+    get_dilution = pltpu.make_async_copy(dilution_hbm, dilution_ref, sems.at[pieces])
+    get_ids = pltpu.make_async_copy(ids_hbm, ids_ref, sems.at[pieces + 1])
+    get_dilution.start()
+    get_ids.start()
+
     row_id = lax.broadcasted_iota(jnp.int32, (16, 2 * width), 0)
     lane_id = lax.broadcasted_iota(jnp.int32, (16, 2 * width), 1)
-    ones = jnp.where(lane_id // LANES == row_id, 1.0, 0.0) * jnp.where(row_id < COLOURS, 1.0, 0.0)
+    ones = jnp.where((lane_id // LANES == row_id) & (row_id < COLOURS), 1.0, 0.0)
     left_ref[pl.ds(total, 16), :] = ones.astype(jnp.bfloat16)
+
+    for piece in range(pieces):
+        copies[piece].wait()
+        there = pl.ds(piece * span, span)
+        flat_ref[there, :] = block_ref[there, :].astype(jnp.float32)
+        for spin in range(SPINS):
+            here = pl.ds(spin * count + piece * batch, batch)
+            for part in range(2):
+                for colour in range(COLOURS):
+                    start = piece * span + (spin * COLOURS + colour) * 2 + part
+                    value = flat_ref[pl.ds(start, batch, stride=2 * comps), :]
+                    lanes = pl.ds(part * width + colour * LANES, LANES)
+                    other = pl.ds((1 - part) * width + colour * LANES, LANES)
+                    left_ref[here, lanes] = value.astype(jnp.bfloat16)
+                    right_ref[here, other] = (value if part else -value).astype(jnp.bfloat16)
+
     dims = (((1,), (1,)), ((), ()))
     real = lax.dot_general(
         left_ref[...], left_ref[pl.ds(0, total), :], dims, preferred_element_type=jnp.float32
     )
     imag = lax.dot_general(left_ref[...], right_ref[...], dims, preferred_element_type=jnp.float32)
-    columns = total // LANES
-    for spin in range(SPINS):
+
+    wide_high = lax.broadcasted_iota(jnp.int32, (rows, LANES), 1) >= count
+    for pair in range(2):
         for column in range(columns):
-            r = real[spin * count : (spin + 1) * count, column * LANES : (column + 1) * LANES]
-            i = imag[spin * count : (spin + 1) * count, column * LANES : (column + 1) * LANES]
-            pair_ref[0, spin, column] = r + i
-            pair_ref[1, spin, column] = r - i
-
+            across = slice(column * LANES, (column + 1) * LANES)
+            blocks = []
+            for spin in (2 * pair, 2 * pair + 1):
+                down = slice(spin * count, (spin + 1) * count)
+                r, i = real[down, across], imag[down, across]
+                blocks.append((r + i, r - i))
+            for kind in range(2):
+                even, odd = blocks[0][kind], blocks[1][kind]
+                for low in range(2):
+                    first, second = (odd, even) if low else (even, odd)
+                    kept = jnp.where(wide_high, second[rows:], first[:rows])
+                    moved = jnp.where(wide_high, second[:rows], first[rows:])
+                    kept_ref[kind, low, pair, column, 0] = kept
+                    kept_ref[kind, low, pair, column, 1] = half_swap(moved, count)
+
+    get_dilution.wait()
     lane = lax.broadcasted_iota(jnp.int32, (1, LANES), 1)
     high = lane >= count
     half = high.astype(jnp.int32)
@@ -166,7 +208,7 @@
         loop_ref[0, mask] = jnp.where(high, found[1], found[0])
         loop_ref[1, mask] = jnp.where(high, found[0], -found[1])
 
-    wide_high = lax.broadcasted_iota(jnp.int32, (rows, LANES), 1) >= count
+    get_ids.wait()
     for place, owner in enumerate(order):
         number = ids_ref[owner]
         imaginary, anti = bit(IMAGINARY, number), bit(ANTI, number)
@@ -174,32 +216,30 @@
         signs = [1 - 2 * bit(NEGATIVE[a], number) for a in range(4)]
         turn = 1 - 2 * (anti & (1 - imaginary))
         kind = imaginary ^ anti
-        odd = wide_high.astype(jnp.int32) == low
-        halves = []
-        for top in range(2):
-            here = pl.ds(top * rows, rows)
-            gathered = None
-            for pair in range(2):
-                column = upper ^ pair
-                even_sign = (signs[2 * pair] * turn).astype(jnp.float32)
-                odd_sign = (signs[2 * pair + 1] * turn).astype(jnp.float32)
-                term = jnp.where(
-                    odd,
-                    even_sign * pair_ref[kind, 2 * pair, column, here, :],
-                    odd_sign * pair_ref[kind, 2 * pair + 1, column, here, :],
-                )
-                gathered = term if gathered is None else gathered + term
-            halves.append(gathered)
-        kept = jnp.where(wide_high, halves[1], halves[0])
-        moved = jnp.where(wide_high, halves[0], halves[1])
+        packed = None
+        for pair in range(2):
+            even, odd = signs[2 * pair] * turn, signs[2 * pair + 1] * turn
+            first = jnp.where(low == 1, odd, even).astype(jnp.float32)
+            second = jnp.where(low == 1, even, odd).astype(jnp.float32)
+            column = upper ^ pair
+            term = jnp.where(wide_high, second, first) * kept_ref[kind, low, pair, column, 0]
+            term += jnp.where(wide_high, first, second) * kept_ref[kind, low, pair, column, 1]
+            packed = term if packed is None else packed + term
         base = place * (rows + 1)
-        out_ref[pl.ds(base, rows), :] = kept + half_swap(moved, count)
+        out_ref[pl.ds(base, rows), :] = packed
         sign = jnp.zeros((1, LANES), jnp.int32)
         for a in range(4):
             sign = jnp.where(spin_of == a, signs[a], sign)
         mask = low + 2 * upper
         out_ref[pl.ds(base + rows, 1), :] = sign.astype(jnp.float32) * loop_ref[imaginary, mask]
 
+    anti = bit(ANTI, ids_ref[lax.axis_index("space")])
+    time_class = index // comps
+    own = lax.axis_index("tm")
+    notes_ref[pl.ds(0, 1), :] = jnp.full((1, LANES), anti, jnp.int32).astype(jnp.float32)
+    notes_ref[pl.ds(1, 1), :] = jnp.where(time_class == own % TDIL, loop_scale, 0.0)
+    notes_ref[pl.ds(2, 1), :] = jnp.where(time_class == (1 - own) % TDIL, loop_scale, 0.0)
+
 
 def sum_kernel(chunks, rows, parts_ref, out_ref):
     total = parts_ref[pl.ds(0, rows), :]
@@ -208,15 +248,13 @@
     out_ref[...] = total
 
 
-def finish_kernel(count, gram_scale, loop_scale, ids_ref, dilution_ref, mine_ref, other_ref, gram_ref, loop_ref):
+def finish_kernel(count, gram_scale, notes_ref, mine_ref, other_ref, gram_ref, loop_ref):
     rows = count // 2
     own = lax.axis_index("tm")
-    number = ids_ref[lax.axis_index("space")]
-    anti = bit(ANTI, number)
+    anti = notes_ref[pl.ds(0, 1), :] > 0.5
     high = lax.broadcasted_iota(jnp.int32, (rows, LANES), 1) >= count
     full_high = lax.broadcasted_iota(jnp.int32, (count, LANES), 1) >= count
-    time_class = dilution_ref[...] // (SPINS * COLOURS)
-    for ref, slice_index in ((mine_ref, own), (other_ref, 1 - own)):
+    for place, (ref, slice_index) in enumerate(((mine_ref, own), (other_ref, 1 - own))):
         packed = ref[pl.ds(0, rows), :]
         swapped = half_swap(packed, count)
         square = jnp.concatenate(
@@ -227,11 +265,10 @@
         imag = (square - turned) * (0.5 * gram_scale)
         plain = jnp.where(full_high, imag, real)
         rotated = jnp.where(full_high, real, -imag)
-        gram_ref[slice_index] = jnp.where(anti == 1, rotated, plain)
-        row = ref[pl.ds(rows, 1), :] * loop_scale
+        gram_ref[slice_index] = jnp.where(anti, rotated, plain)
+        row = ref[pl.ds(rows, 1), :] * notes_ref[pl.ds(1 + place, 1), :]
         both = jnp.concatenate([row, half_swap(row, count)], axis=0)
-        live = (time_class == slice_index % TDIL).astype(jnp.float32)
-        loop_ref[slice_index] = both[:, :count] * live
+        loop_ref[slice_index] = both[:, :count]
 
 
 def packed_shards(vectors, dilution, gamma_ids):
@@ -245,23 +282,31 @@
     chunk = rows + 1
     block = jnp.transpose(vectors, (0, 1, 3, 2, 4)).reshape(count * comps * halves, sites)
     vmem = pl.BlockSpec(memory_space=pltpu.VMEM)
-    smem = pl.BlockSpec(memory_space=pltpu.SMEM)
+    hbm = pl.BlockSpec(memory_space=pltpu.HBM)
     total = SPINS * count
-    parts = pl.pallas_call(
-        partial(partial_kernel, count, order),
-        out_shape=jax.ShapeDtypeStruct((owners * chunk, LANES), jnp.float32),
-        in_specs=[smem, vmem, vmem],
-        out_specs=vmem,
+    width = halves * COLOURS * LANES
+    parts, notes = pl.pallas_call(
+        partial(partial_kernel, count, order, loop_scale),
+        out_shape=(
+            jax.ShapeDtypeStruct((owners * chunk, LANES), jnp.float32),
+            jax.ShapeDtypeStruct((8, LANES), jnp.float32),
+        ),
+        in_specs=[hbm, hbm, hbm],
+        out_specs=(vmem, vmem),
         scratch_shapes=[
-            pltpu.VMEM((count * comps * halves, LANES), jnp.float32),
-            pltpu.VMEM((total + 16, 2 * COLOURS * LANES), jnp.bfloat16),
-            pltpu.VMEM((total, 2 * COLOURS * LANES), jnp.bfloat16),
-            pltpu.VMEM((2, SPINS, total // LANES, count, LANES), jnp.float32),
+            pltpu.SMEM(gamma_ids.shape, jnp.int32),
+            pltpu.VMEM((1, count), jnp.int32),
+            pltpu.VMEM(block.shape, block.dtype),
+            pltpu.VMEM(block.shape, jnp.float32),
+            pltpu.VMEM((total + 16, width), jnp.bfloat16),
+            pltpu.VMEM((total, width), jnp.bfloat16),
+            pltpu.VMEM((2, 2, 2, total // LANES, 2, rows, LANES), jnp.float32),
             pltpu.VMEM((2, 4, 1, LANES), jnp.float32),
+            pltpu.SemaphoreType.DMA((PIECES + 2,)),
         ],
         compiler_params=pltpu.CompilerParams(vmem_limit_bytes=16 << 20),
         name="partial_gram",
-    )(gamma_ids, dilution.reshape(1, count), block)
+    )(*(in_hbm(v) for v in (gamma_ids, dilution.reshape(1, count), block)))
     swapped = lax.all_to_all(
         parts.reshape(owners, chunk, 1, LANES),
         "space",
@@ -280,16 +325,16 @@
     )(swapped.reshape(owners * chunk, LANES))
     other = lax.ppermute(mine, "tm", [(0, 1), (1, 0)])
     gram, loops = pl.pallas_call(
-        partial(finish_kernel, count, gram_scale, loop_scale),
+        partial(finish_kernel, count, gram_scale),
         out_shape=(
             jax.ShapeDtypeStruct((2, count, LANES), jnp.float32),
             jax.ShapeDtypeStruct((2, 2, count), jnp.float32),
         ),
-        in_specs=[smem, vmem, vmem, vmem],
+        in_specs=[vmem, vmem, vmem],
         out_specs=(vmem, vmem),
         compiler_params=pltpu.CompilerParams(vmem_limit_bytes=4 << 20),
         name="finish",
-    )(gamma_ids, dilution.reshape(1, count), mine, other)
+    )(notes, mine, other)
     return gram, jnp.transpose(loops, (0, 2, 1))
 
 

time: 22.5 us -> 20.5 us (0.911)
  local copies, waits for them, and re-layouts: 1.65 us -> 0 us
  blocking collectives: 16 us -> 15.5 us
    unnamed x6 -> x0, local copies, waits for them, and re-layouts: 1.65 us -> none
    all_to_all x1, blocking collectives: 16 us -> 15.5 us  [packed_shards(): lax.all_to_all(parts.reshape(owners, chunk, 1, LANES), 'space', 0, 0, til...]
where the time goes in v2:
time: 20.5 us; the launch traced here: 20.3 us
  blocking collectives  15.5 us (76%)
  Pallas kernels  2.94 us (14%)
  waiting for transfers between devices  1.18 us (6%)
  between operations  0.65 us (3%)
    all_to_all x1, blocking collectives, packed_shards(): lax.all_to_all(parts.reshape(owners, chunk, 1, LANES), 'space', 0, 0, til...  15.5 us
    pallas_call x1, Pallas kernels, packed_shards(): pl.pallas_call(partial(partial_kernel, count, order, loop_scale), out_sha...  2.12 us
    ppermute x1, waiting for transfers between devices, packed_shards(): other = lax.ppermute(mine, 'tm', [(0, 1), (1, 0)])  1.18 us
    pallas_call x1, Pallas kernels, packed_shards(): pl.pallas_call(partial(finish_kernel, count, gram_scale), out_shape=(jax....  0.79 us
  transfers between devices with their start and end apart: 1, of which 1 were waited for; matrix products, arithmetic and copies ran while one was open for 0% of the time, Pallas kernels for 0%

profile of v2, /device:TPU:0, one launch (start us, length us, event | category | flops | bytes accessed | tf_op | source)
XLA Modules:
  0.0 20.3 jit_solution(1720375620130619411)
XLA Ops:
  0.6 2.1 %partial_gram.1 = (f32[528,128]{1,0:T(8,128)S(1)}, f32[8,128]{1,0:T(8,128)S(1)}) custom-call(s32[16]{0:T(128)} %ids_hbm.1, s32[1,64]{1,0:T(1,128)} %bitcast.10, bf16[1536,128]{1,0:T(8,128)(2,1)} %bitcast.9), custom_call_target="tpu_custom_call" | custom-call | tf_op jit(solution)/shard_map/partial_gram/pallas_call | solution.py:288
  2.8 15.5 %all_to_all.5 = f32[16,33,1,128]{3,2,1,0:T(1,128)S(1)} all-to-all(f32[16,33,1,128]{3,2,1,0:T(1,128)S(1)} %bitcast.8), channel_id=1, replica_groups={{16,2,14,20,28,30,26,8,18,22,10,4,24,0,12,6},{17,3,15,21,29,31,27,9,19,..., dimensions={0} | all-to-all | bytes 540672 | tf_op jit(solution)/shard_map/all_to_all | solution.py:310
  18.3 0.1 collective-permute-start
  18.3 1.2 %collective-permute-done.other_ref = f32[33,128]{1,0:T(8,128)S(1)} collective-permute-done((f32[33,128]{1,0:T(8,128)S(1)}, f32[33,128]{1,0:T(8,128)S(1)}, u32[]{:S(2)}, u32[]{:S(2)}) %collective-permute-start) | collective-permute-done | bytes 16928 | tf_op jit(solution)/shard_map/ppermute | solution.py:326
  19.5 0.8 %finish.1 = (f32[2,64,128]{2,1,0:T(8,128)}, f32[2,2,64]{2,1,0:T(2,128)}) custom-call(f32[8,128]{1,0:T(8,128)S(1)} %get-tuple-element.6.notes_ref, f32[33,128]{1,0:T(8,128)S(1)} %sum_chunks.1.mine_ref, f32[33,128]{1,0:T(8,128)S(1)} %collective-permute-done.other_ref), custom_call_target="tpu_custom_call" | custom-call | tf_op jit(solution)/shard_map/finish/pallas_call | solution.py:327
  (1 shorter events, 0.0 us)
Async XLA Ops:
  18.3 1.3 %collective-permute-start = (f32[33,128]{1,0:T(8,128)S(1)}, f32[33,128]{1,0:T(8,128)S(1)}, u32[]{:S(2)}, u32[]{:S(2)}) collective-permute-start(f32[33,128]{1,0:T(8,128)S(1)} %sum_chunks.1.mine_ref), channel_id=1, source_target_pairs={{0,1},{1,0},{2,3},{3,2},{4,5},{5,4},{6,7},{7,6},{8,9},{9,8},{10,11... | collective-permute-start | bytes 50696 | tf_op jit(solution)/shard_map/ppermute | solution.py:326

commit v3 on v2

--- a/solution.py
+++ b/solution.py
@@ -12,9 +12,11 @@
 SPINS = 4
 COLOURS = 3
 LANES = 128
-PIECES = 4
-
-EXCHANGE_ORDER = (8, 1, 7, 10, 14, 15, 13, 4, 9, 11, 5, 2, 12, 0, 6, 3)
+
+EXCHANGE_ORDERS = (
+    (11, 1, 14, 7, 2, 8, 4, 13, 0, 6, 3, 5, 15, 9, 10, 12),
+    (9, 8, 0, 10, 15, 4, 1, 3, 5, 2, 11, 12, 6, 7, 13, 14),
+)
 
 
 highest = lax.Precision.HIGHEST
@@ -60,33 +62,24 @@
     return squares
 
 
-def dirac_bits():
-    imaginary, anti, mask_low, mask_high = 0, 0, 0, 0
-    negative = [0, 0, 0, 0]
-    for number, (real, imag) in enumerate(dirac_squares()):
-        places = [[b for b in range(4) if real[a][b] or imag[a][b]] for a in range(4)]
-        mask = places[0][0]
-        assert all(places[a] == [a ^ mask] for a in range(4))
-        kind = int(imag[0][mask] != 0)
-        values = [(imag if kind else real)[a][a ^ mask] for a in range(4)]
+def dirac_entries():
+    entries = []
+    for real, imag in dirac_squares():
+        mask = next(b for b in range(4) if real[0][b] or imag[0][b])
+        imaginary = int(imag[0][mask] != 0)
+        square, other = (imag, real) if imaginary else (real, imag)
+        values = [square[a][a ^ mask] for a in range(4)]
         assert all(abs(v) == 1 for v in values)
-        sign = -1 if kind else 1
-        flips = {values[a] * values[a ^ mask] * sign for a in range(4)}
+        assert sum(abs(v) for line in square for v in line) == 4
+        assert not any(v for line in other for v in line)
+        flips = {values[a] * values[a ^ mask] * (-1 if imaginary else 1) for a in range(4)}
         assert len(flips) == 1
-        imaginary |= kind << number
-        anti |= int(flips == {-1}) << number
-        mask_low |= (mask & 1) << number
-        mask_high |= (mask >> 1) << number
-        for a in range(4):
-            negative[a] |= int(values[a] < 0) << number
-    return imaginary, anti, mask_low, mask_high, negative
-
-
-IMAGINARY, ANTI, MASK_LOW, MASK_HIGH, NEGATIVE = dirac_bits()
-
-
-def bit(word, number):
-    return (jnp.int32(word) >> number) & 1
+        entries.append((imaginary, int(flips == {-1}), mask, tuple(values)))
+    return entries
+
+
+GAMMAS = dirac_entries()
+ANTI = sum(entry[1] << number for number, entry in enumerate(GAMMAS))
 
 
 def pick_gammas(gamma_ids):
@@ -112,83 +105,59 @@
 
 
 def partial_kernel(
-    count, order, loop_scale, ids_hbm, dilution_hbm, block_hbm, out_ref, notes_ref,
-    ids_ref, dilution_ref, block_ref, flat_ref, left_ref, right_ref, kept_ref, loop_ref, sems,
+    count, orders, loop_scale, ids_hbm, dilution_hbm, block_hbm, out_ref, notes_ref,
+    ids_ref, dilution_ref, block_ref, flat_ref, gram_ref, loop_ref, sems,
 ):
     comps = SPINS * COLOURS
-    width = COLOURS * LANES
     rows = count // 2
     total = SPINS * count
     columns = total // LANES
-    pieces = PIECES
-    batch = count // pieces
-    span = batch * comps * 2
-    copies = [
-        pltpu.make_async_copy(
-            block_hbm.at[pl.ds(piece * span, span), :],
-            block_ref.at[pl.ds(piece * span, span), :],
-            sems.at[piece],
-        )
-        for piece in range(pieces)
-    ]
-    for copy in copies:
-        copy.start()
-    get_dilution = pltpu.make_async_copy(dilution_hbm, dilution_ref, sems.at[pieces])
-    get_ids = pltpu.make_async_copy(ids_hbm, ids_ref, sems.at[pieces + 1])
+    get_block = pltpu.make_async_copy(block_hbm, block_ref, sems.at[0])
+    get_dilution = pltpu.make_async_copy(dilution_hbm, dilution_ref, sems.at[1])
+    get_ids = pltpu.make_async_copy(ids_hbm, ids_ref, sems.at[2])
+    get_block.start()
     get_dilution.start()
     get_ids.start()
 
-    row_id = lax.broadcasted_iota(jnp.int32, (16, 2 * width), 0)
-    lane_id = lax.broadcasted_iota(jnp.int32, (16, 2 * width), 1)
-    ones = jnp.where((lane_id // LANES == row_id) & (row_id < COLOURS), 1.0, 0.0)
-    left_ref[pl.ds(total, 16), :] = ones.astype(jnp.bfloat16)
-
-    for piece in range(pieces):
-        copies[piece].wait()
-        there = pl.ds(piece * span, span)
-        flat_ref[there, :] = block_ref[there, :].astype(jnp.float32)
-        for spin in range(SPINS):
-            here = pl.ds(spin * count + piece * batch, batch)
-            for part in range(2):
-                for colour in range(COLOURS):
-                    start = piece * span + (spin * COLOURS + colour) * 2 + part
-                    value = flat_ref[pl.ds(start, batch, stride=2 * comps), :]
-                    lanes = pl.ds(part * width + colour * LANES, LANES)
-                    other = pl.ds((1 - part) * width + colour * LANES, LANES)
-                    left_ref[here, lanes] = value.astype(jnp.bfloat16)
-                    right_ref[here, other] = (value if part else -value).astype(jnp.bfloat16)
-
-    dims = (((1,), (1,)), ((), ()))
-    real = lax.dot_general(
-        left_ref[...], left_ref[pl.ds(0, total), :], dims, preferred_element_type=jnp.float32
-    )
-    imag = lax.dot_general(left_ref[...], right_ref[...], dims, preferred_element_type=jnp.float32)
-
-    wide_high = lax.broadcasted_iota(jnp.int32, (rows, LANES), 1) >= count
-    for pair in range(2):
-        for column in range(columns):
-            across = slice(column * LANES, (column + 1) * LANES)
-            blocks = []
-            for spin in (2 * pair, 2 * pair + 1):
-                down = slice(spin * count, (spin + 1) * count)
-                r, i = real[down, across], imag[down, across]
-                blocks.append((r + i, r - i))
-            for kind in range(2):
-                even, odd = blocks[0][kind], blocks[1][kind]
-                for low in range(2):
-                    first, second = (odd, even) if low else (even, odd)
-                    kept = jnp.where(wide_high, second[rows:], first[:rows])
-                    moved = jnp.where(wide_high, second[:rows], first[rows:])
-                    kept_ref[kind, low, pair, column, 0] = kept
-                    kept_ref[kind, low, pair, column, 1] = half_swap(moved, count)
-
     get_dilution.wait()
+    get_ids.wait()
     lane = lax.broadcasted_iota(jnp.int32, (1, LANES), 1)
     high = lane >= count
     half = high.astype(jnp.int32)
     index = jnp.concatenate([dilution_ref[...]] * 2, axis=1)
     spin_of = index % comps // COLOURS
     colour_of = index % COLOURS
+    time_class = index // comps
+    own = lax.axis_index("tm")
+    mine = ids_ref[lax.axis_index("space")]
+    anti = (jnp.int32(ANTI) >> mine) & 1
+    notes_ref[pl.ds(0, 1), :] = jnp.full((1, LANES), anti, jnp.int32).astype(jnp.float32)
+    notes_ref[pl.ds(1, 1), :] = jnp.where(time_class == own % TDIL, loop_scale, 0.0)
+    notes_ref[pl.ds(2, 1), :] = jnp.where(time_class == (1 - own) % TDIL, loop_scale, 0.0)
+    get_block.wait()
+
+    flat_ref[...] = block_ref[...].astype(jnp.float32)
+    row_id = lax.broadcasted_iota(jnp.int32, (16, 2 * LANES), 0)
+    real_lanes = lax.broadcasted_iota(jnp.int32, (16, 2 * LANES), 1) < LANES
+    both = None
+    for colour in range(COLOURS):
+        parts = []
+        for part in range(2):
+            starts = [(spin * COLOURS + colour) * 2 + part for spin in range(SPINS)]
+            pieces = [flat_ref[pl.ds(start, count, stride=2 * comps), :] for start in starts]
+            parts.append(jnp.concatenate(pieces, axis=0).astype(jnp.bfloat16))
+        spinor = jnp.concatenate(parts, axis=1)
+        turned = jnp.concatenate([parts[1], -parts[0]], axis=1)
+        ones = jnp.where((row_id == colour) & real_lanes, 1.0, 0.0).astype(jnp.bfloat16)
+        term = lax.dot_general(
+            jnp.concatenate([spinor, ones], axis=0),
+            jnp.concatenate([turned, spinor], axis=0),
+            (((1,), (1,)), ((), ())),
+            preferred_element_type=jnp.float32,
+        )
+        both = term if both is None else both + term
+    imag, real = both[:, :total], both[:, total:]
+
     sums = []
     for grid in (real, imag):
         for column in range(columns):
@@ -205,40 +174,64 @@
             value = jnp.where(source >= 2, upper, lower)
             value = jnp.where((source & 1) == half, value, 0.0)
             found.append(value + half_swap(value, count))
-        loop_ref[0, mask] = jnp.where(high, found[1], found[0])
-        loop_ref[1, mask] = jnp.where(high, found[0], -found[1])
-
-    get_ids.wait()
-    for place, owner in enumerate(order):
-        number = ids_ref[owner]
-        imaginary, anti = bit(IMAGINARY, number), bit(ANTI, number)
-        low, upper = bit(MASK_LOW, number), bit(MASK_HIGH, number)
-        signs = [1 - 2 * bit(NEGATIVE[a], number) for a in range(4)]
-        turn = 1 - 2 * (anti & (1 - imaginary))
-        kind = imaginary ^ anti
-        packed = None
+        turned = (jnp.where(high, found[1], found[0]), jnp.where(high, found[0], -found[1]))
+        for number, (imaginary, _, shift, values) in enumerate(GAMMAS):
+            if shift == mask:
+                sign = jnp.full((1, LANES), float(values[0]), jnp.float32)
+                for spin in range(1, SPINS):
+                    sign = jnp.where(spin_of == spin, float(values[spin]), sign)
+                loop_ref[pl.ds(number, 1), :] = sign * turned[imaginary]
+
+    wide_high = lax.broadcasted_iota(jnp.int32, (rows, LANES), 1) >= count
+    tilt = jnp.where(wide_high, -1.0, 1.0)
+    for upper in range(2):
+        blocks = []
         for pair in range(2):
-            even, odd = signs[2 * pair] * turn, signs[2 * pair + 1] * turn
-            first = jnp.where(low == 1, odd, even).astype(jnp.float32)
-            second = jnp.where(low == 1, even, odd).astype(jnp.float32)
             column = upper ^ pair
-            term = jnp.where(wide_high, second, first) * kept_ref[kind, low, pair, column, 0]
-            term += jnp.where(wide_high, first, second) * kept_ref[kind, low, pair, column, 1]
-            packed = term if packed is None else packed + term
+            across = slice(column * LANES, (column + 1) * LANES)
+            pieces = []
+            for spin in (2 * pair, 2 * pair + 1):
+                down = slice(spin * count, (spin + 1) * count)
+                r, i = real[down, across], imag[down, across]
+                pieces.append((r + i, r - i))
+            blocks.append(pieces)
+        for low in range(2):
+            made = {}
+
+            def part_of(kind, pair, same):
+                if (kind, pair) not in made:
+                    even, odd = blocks[pair][0][kind], blocks[pair][1][kind]
+                    first, second = (odd, even) if low else (even, odd)
+                    kept = jnp.where(wide_high, second[rows:], first[:rows])
+                    moved = half_swap(jnp.where(wide_high, second[:rows], first[rows:]), count)
+                    made[kind, pair] = (kept, moved)
+                kept, moved = made[kind, pair]
+                if (kind, pair, same) not in made:
+                    made[kind, pair, same] = kept + moved if same else tilt * (kept - moved)
+                return made[kind, pair, same]
+
+            for number, (imaginary, anti_one, shift, values) in enumerate(GAMMAS):
+                if shift != low + 2 * upper:
+                    continue
+                kind = imaginary ^ anti_one
+                turn = -1 if anti_one and not imaginary else 1
+                terms = []
+                for pair in range(2):
+                    first = turn * values[2 * pair + low]
+                    second = turn * values[2 * pair + 1 - low]
+                    terms.append((first, part_of(kind, pair, first == second)))
+                (one, left), (two, right) = terms
+                if one > 0:
+                    value = left + right if two > 0 else left - right
+                else:
+                    value = right - left if two > 0 else -(left + right)
+                gram_ref[number] = value
+
+    for place, owners in enumerate(zip(*orders)):
+        number = ids_ref[jnp.where(own == 0, *owners)]
         base = place * (rows + 1)
-        out_ref[pl.ds(base, rows), :] = packed
-        sign = jnp.zeros((1, LANES), jnp.int32)
-        for a in range(4):
-            sign = jnp.where(spin_of == a, signs[a], sign)
-        mask = low + 2 * upper
-        out_ref[pl.ds(base + rows, 1), :] = sign.astype(jnp.float32) * loop_ref[imaginary, mask]
-
-    anti = bit(ANTI, ids_ref[lax.axis_index("space")])
-    time_class = index // comps
-    own = lax.axis_index("tm")
-    notes_ref[pl.ds(0, 1), :] = jnp.full((1, LANES), anti, jnp.int32).astype(jnp.float32)
-    notes_ref[pl.ds(1, 1), :] = jnp.where(time_class == own % TDIL, loop_scale, 0.0)
-    notes_ref[pl.ds(2, 1), :] = jnp.where(time_class == (1 - own) % TDIL, loop_scale, 0.0)
+        out_ref[pl.ds(base, rows), :] = gram_ref[number]
+        out_ref[pl.ds(base + rows, 1), :] = loop_ref[pl.ds(number, 1), :]
 
 
 def sum_kernel(chunks, rows, parts_ref, out_ref):
@@ -277,16 +270,16 @@
     total_sites = sites * owners
     gram_scale = 1.0 / math.sqrt(48.0 * total_sites)
     loop_scale = 1.0 / math.sqrt(1.0 * total_sites)
-    order = EXCHANGE_ORDER if owners == len(EXCHANGE_ORDER) else tuple(range(owners))
+    orders = EXCHANGE_ORDERS
+    if any(len(order) != owners for order in orders):
+        orders = (tuple(range(owners)),) * 2
     rows = count // 2
     chunk = rows + 1
     block = jnp.transpose(vectors, (0, 1, 3, 2, 4)).reshape(count * comps * halves, sites)
     vmem = pl.BlockSpec(memory_space=pltpu.VMEM)
     hbm = pl.BlockSpec(memory_space=pltpu.HBM)
-    total = SPINS * count
-    width = halves * COLOURS * LANES
     parts, notes = pl.pallas_call(
-        partial(partial_kernel, count, order, loop_scale),
+        partial(partial_kernel, count, orders, loop_scale),
         out_shape=(
             jax.ShapeDtypeStruct((owners * chunk, LANES), jnp.float32),
             jax.ShapeDtypeStruct((8, LANES), jnp.float32),
@@ -298,22 +291,20 @@
             pltpu.VMEM((1, count), jnp.int32),
             pltpu.VMEM(block.shape, block.dtype),
             pltpu.VMEM(block.shape, jnp.float32),
-            pltpu.VMEM((total + 16, width), jnp.bfloat16),
-            pltpu.VMEM((total, width), jnp.bfloat16),
-            pltpu.VMEM((2, 2, 2, total // LANES, 2, rows, LANES), jnp.float32),
-            pltpu.VMEM((2, 4, 1, LANES), jnp.float32),
-            pltpu.SemaphoreType.DMA((PIECES + 2,)),
+            pltpu.VMEM((len(GAMMAS), rows, LANES), jnp.float32),
+            pltpu.VMEM((len(GAMMAS), LANES), jnp.float32),
+            pltpu.SemaphoreType.DMA((3,)),
         ],
         compiler_params=pltpu.CompilerParams(vmem_limit_bytes=16 << 20),
         name="partial_gram",
     )(*(in_hbm(v) for v in (gamma_ids, dilution.reshape(1, count), block)))
     swapped = lax.all_to_all(
         parts.reshape(owners, chunk, 1, LANES),
-        "space",
+        ("space", "tm"),
         0,
         0,
         tiled=True,
-        axis_index_groups=[list(order)],
+        axis_index_groups=[[2 * owner + core for owner in orders[core]] for core in range(2)],
     )
     mine = pl.pallas_call(
         partial(sum_kernel, owners, chunk),

time: 20.5 us -> 19.4 us (0.946)
  blocking collectives: 15.5 us -> 14.9 us
  Pallas kernels: 2.94 us -> 2.42 us
    all_to_all x1, blocking collectives: 15.5 us -> 14.9 us  [packed_shards(): lax.all_to_all(parts.reshape(owners, chunk, 1, LANES), ('space', 'tm'), 0...]
    pallas_call x1, Pallas kernels: 2.12 us -> 1.6 us  [packed_shards(): pl.pallas_call(partial(partial_kernel, count, orders, loop_scale), out_sh...]
where the time goes in v3:
time: 19.4 us; the launch traced here: 19.2 us
  blocking collectives  14.9 us (77%)
  Pallas kernels  2.42 us (12%)
  waiting for transfers between devices  1.18 us (6%)
  between operations  0.65 us (3%)
    all_to_all x1, blocking collectives, packed_shards(): lax.all_to_all(parts.reshape(owners, chunk, 1, LANES), ('space', 'tm'), 0...  14.9 us
    pallas_call x1, Pallas kernels, packed_shards(): pl.pallas_call(partial(partial_kernel, count, orders, loop_scale), out_sh...  1.6 us
    ppermute x1, waiting for transfers between devices, packed_shards(): other = lax.ppermute(mine, 'tm', [(0, 1), (1, 0)])  1.18 us
    pallas_call x1, Pallas kernels, packed_shards(): pl.pallas_call(partial(finish_kernel, count, gram_scale), out_shape=(jax....  0.79 us
  transfers between devices with their start and end apart: 1, of which 1 were waited for; matrix products, arithmetic and copies ran while one was open for 0% of the time, Pallas kernels for 0%

profile of v3, /device:TPU:0, one launch (start us, length us, event | category | flops | bytes accessed | tf_op | source)
XLA Modules:
  0.0 19.2 jit_solution(16138988509822390071)
XLA Ops:
  0.6 1.6 %partial_gram.1 = (f32[528,128]{1,0:T(8,128)S(1)}, f32[8,128]{1,0:T(8,128)S(1)}) custom-call(s32[16]{0:T(128)} %ids_hbm.1, s32[1,64]{1,0:T(1,128)} %bitcast.10, bf16[1536,128]{1,0:T(8,128)(2,1)} %bitcast.9), custom_call_target="tpu_custom_call" | custom-call | tf_op jit(solution)/shard_map/partial_gram/pallas_call | solution.py:281
  2.2 14.9 %all_to_all.5 = f32[16,33,1,128]{3,2,1,0:T(1,128)S(1)} all-to-all(f32[16,33,1,128]{3,2,1,0:T(1,128)S(1)} %bitcast.8), channel_id=1, replica_groups={{22,2,28,14,4,16,8,26,0,12,6,10,30,18,20,24},{19,17,1,21,31,9,3,7,11,5,..., dimensions={0} | all-to-all | bytes 540672 | tf_op jit(solution)/shard_map/all_to_all | solution.py:301
  17.2 0.1 collective-permute-start
  17.3 1.2 %collective-permute-done.other_ref = f32[33,128]{1,0:T(8,128)S(1)} collective-permute-done((f32[33,128]{1,0:T(8,128)S(1)}, f32[33,128]{1,0:T(8,128)S(1)}, u32[]{:S(2)}, u32[]{:S(2)}) %collective-permute-start) | collective-permute-done | bytes 16928 | tf_op jit(solution)/shard_map/ppermute | solution.py:317
  18.4 0.8 %finish.1 = (f32[2,64,128]{2,1,0:T(8,128)}, f32[2,2,64]{2,1,0:T(2,128)}) custom-call(f32[8,128]{1,0:T(8,128)S(1)} %get-tuple-element.6.notes_ref, f32[33,128]{1,0:T(8,128)S(1)} %sum_chunks.1.mine_ref, f32[33,128]{1,0:T(8,128)S(1)} %collective-permute-done.other_ref), custom_call_target="tpu_custom_call" | custom-call | tf_op jit(solution)/shard_map/finish/pallas_call | solution.py:318
  (1 shorter events, 0.0 us)
Async XLA Ops:
  17.2 1.3 %collective-permute-start = (f32[33,128]{1,0:T(8,128)S(1)}, f32[33,128]{1,0:T(8,128)S(1)}, u32[]{:S(2)}, u32[]{:S(2)}) collective-permute-start(f32[33,128]{1,0:T(8,128)S(1)} %sum_chunks.1.mine_ref), channel_id=1, source_target_pairs={{0,1},{1,0},{2,3},{3,2},{4,5},{5,4},{6,7},{7,6},{8,9},{9,8},{10,11... | collective-permute-start | bytes 50696 | tf_op jit(solution)/shard_map/ppermute | solution.py:317

commit v4 on v3

--- a/solution.py
+++ b/solution.py
@@ -14,8 +14,8 @@
 LANES = 128
 
 EXCHANGE_ORDERS = (
-    (11, 1, 14, 7, 2, 8, 4, 13, 0, 6, 3, 5, 15, 9, 10, 12),
-    (9, 8, 0, 10, 15, 4, 1, 3, 5, 2, 11, 12, 6, 7, 13, 14),
+    (15, 8, 14, 11, 5, 6, 12, 4, 9, 0, 2, 1, 13, 10, 7, 3),
+    (11, 9, 12, 1, 2, 15, 13, 6, 0, 10, 5, 8, 3, 7, 4, 14),
 )
 
 

time: 19.4 us -> 18.9 us (0.974)
  blocking collectives: 14.9 us -> 14.4 us
    all_to_all x1, blocking collectives: 14.9 us -> 14.4 us  [packed_shards(): lax.all_to_all(parts.reshape(owners, chunk, 1, LANES), ('space', 'tm'), 0...]
where the time goes in v4:
time: 18.9 us; the launch traced here: 18.8 us
  blocking collectives  14.4 us (76%)
  Pallas kernels  2.42 us (13%)
  waiting for transfers between devices  1.18 us (6%)
  between operations  0.65 us (3%)
    all_to_all x1, blocking collectives, packed_shards(): lax.all_to_all(parts.reshape(owners, chunk, 1, LANES), ('space', 'tm'), 0...  14.4 us
    pallas_call x1, Pallas kernels, packed_shards(): pl.pallas_call(partial(partial_kernel, count, orders, loop_scale), out_sh...  1.6 us
    ppermute x1, waiting for transfers between devices, packed_shards(): other = lax.ppermute(mine, 'tm', [(0, 1), (1, 0)])  1.18 us
    pallas_call x1, Pallas kernels, packed_shards(): pl.pallas_call(partial(finish_kernel, count, gram_scale), out_shape=(jax....  0.79 us
  transfers between devices with their start and end apart: 1, of which 1 were waited for; matrix products, arithmetic and copies ran while one was open for 0% of the time, Pallas kernels for 0%

profile of v4, /device:TPU:0, one launch (start us, length us, event | category | flops | bytes accessed | tf_op | source)
XLA Modules:
  0.0 18.8 jit_solution(9402755731394522662)
XLA Ops:
  0.6 1.6 %partial_gram.1 = (f32[528,128]{1,0:T(8,128)S(1)}, f32[8,128]{1,0:T(8,128)S(1)}) custom-call(s32[16]{0:T(128)} %ids_hbm.1, s32[1,64]{1,0:T(1,128)} %bitcast.10, bf16[1536,128]{1,0:T(8,128)(2,1)} %bitcast.9), custom_call_target="tpu_custom_call" | custom-call | tf_op jit(solution)/shard_map/partial_gram/pallas_call | solution.py:281
  2.2 14.4 %all_to_all.5 = f32[16,33,1,128]{3,2,1,0:T(1,128)S(1)} all-to-all(f32[16,33,1,128]{3,2,1,0:T(1,128)S(1)} %bitcast.8), channel_id=1, replica_groups={{30,16,28,22,10,12,24,8,18,0,4,2,26,20,14,6},{23,19,25,3,5,31,27,13,1,2..., dimensions={0} | all-to-all | bytes 540672 | tf_op jit(solution)/shard_map/all_to_all | solution.py:301
  16.7 0.1 collective-permute-start
  16.8 1.2 %collective-permute-done.other_ref = f32[33,128]{1,0:T(8,128)S(1)} collective-permute-done((f32[33,128]{1,0:T(8,128)S(1)}, f32[33,128]{1,0:T(8,128)S(1)}, u32[]{:S(2)}, u32[]{:S(2)}) %collective-permute-start) | collective-permute-done | bytes 16928 | tf_op jit(solution)/shard_map/ppermute | solution.py:317
  18.0 0.8 %finish.1 = (f32[2,64,128]{2,1,0:T(8,128)}, f32[2,2,64]{2,1,0:T(2,128)}) custom-call(f32[8,128]{1,0:T(8,128)S(1)} %get-tuple-element.6.notes_ref, f32[33,128]{1,0:T(8,128)S(1)} %sum_chunks.1.mine_ref, f32[33,128]{1,0:T(8,128)S(1)} %collective-permute-done.other_ref), custom_call_target="tpu_custom_call" | custom-call | tf_op jit(solution)/shard_map/finish/pallas_call | solution.py:318
  (1 shorter events, 0.0 us)
Async XLA Ops:
  16.7 1.3 %collective-permute-start = (f32[33,128]{1,0:T(8,128)S(1)}, f32[33,128]{1,0:T(8,128)S(1)}, u32[]{:S(2)}, u32[]{:S(2)}) collective-permute-start(f32[33,128]{1,0:T(8,128)S(1)} %sum_chunks.1.mine_ref), channel_id=1, source_target_pairs={{0,1},{1,0},{2,3},{3,2},{4,5},{5,4},{6,7},{7,6},{8,9},{9,8},{10,11... | collective-permute-start | bytes 50696 | tf_op jit(solution)/shard_map/ppermute | solution.py:317

commit v5 on v4

--- a/solution.py
+++ b/solution.py
@@ -14,7 +14,7 @@
 LANES = 128
 
 EXCHANGE_ORDERS = (
-    (15, 8, 14, 11, 5, 6, 12, 4, 9, 0, 2, 1, 13, 10, 7, 3),
+    (13, 8, 14, 11, 5, 6, 15, 4, 9, 0, 2, 1, 12, 10, 7, 3),
     (11, 9, 12, 1, 2, 15, 13, 6, 0, 10, 5, 8, 3, 7, 4, 14),
 )
 
@@ -80,6 +80,7 @@
 
 GAMMAS = dirac_entries()
 ANTI = sum(entry[1] << number for number, entry in enumerate(GAMMAS))
+SWAPPED = sum((entry[0] ^ entry[1]) << number for number, entry in enumerate(GAMMAS))
 
 
 def pick_gammas(gamma_ids):
@@ -130,15 +131,17 @@
     time_class = index // comps
     own = lax.axis_index("tm")
     mine = ids_ref[lax.axis_index("space")]
-    anti = (jnp.int32(ANTI) >> mine) & 1
-    notes_ref[pl.ds(0, 1), :] = jnp.full((1, LANES), anti, jnp.int32).astype(jnp.float32)
-    notes_ref[pl.ds(1, 1), :] = jnp.where(time_class == own % TDIL, loop_scale, 0.0)
-    notes_ref[pl.ds(2, 1), :] = jnp.where(time_class == (1 - own) % TDIL, loop_scale, 0.0)
+    flags = [(jnp.int32(word) >> mine) & 1 for word in (ANTI, SWAPPED)]
+    for row, flag in enumerate(flags):
+        notes_ref[pl.ds(row, 1), :] = jnp.full((1, LANES), flag, jnp.int32).astype(jnp.float32)
+    notes_ref[pl.ds(2, 1), :] = jnp.where(time_class == own % TDIL, loop_scale, 0.0)
+    notes_ref[pl.ds(3, 1), :] = jnp.where(time_class == (1 - own) % TDIL, loop_scale, 0.0)
     get_block.wait()
 
     flat_ref[...] = block_ref[...].astype(jnp.float32)
     row_id = lax.broadcasted_iota(jnp.int32, (16, 2 * LANES), 0)
-    real_lanes = lax.broadcasted_iota(jnp.int32, (16, 2 * LANES), 1) < LANES
+    part_id = lax.broadcasted_iota(jnp.int32, (16, 2 * LANES), 1) // LANES
+    blank = jnp.zeros((16, 2 * LANES), jnp.bfloat16)
     both = None
     for colour in range(COLOURS):
         parts = []
@@ -148,22 +151,23 @@
             parts.append(jnp.concatenate(pieces, axis=0).astype(jnp.bfloat16))
         spinor = jnp.concatenate(parts, axis=1)
         turned = jnp.concatenate([parts[1], -parts[0]], axis=1)
-        ones = jnp.where((row_id == colour) & real_lanes, 1.0, 0.0).astype(jnp.bfloat16)
-        term = lax.dot_general(
-            jnp.concatenate([spinor, ones], axis=0),
-            jnp.concatenate([turned, spinor], axis=0),
-            (((1,), (1,)), ((), ())),
-            preferred_element_type=jnp.float32,
-        )
-        both = term if both is None else both + term
-    imag, real = both[:, :total], both[:, total:]
+        ones = jnp.where(row_id == 2 * colour + part_id, 1.0, 0.0).astype(jnp.bfloat16)
+        for below, right in ((ones, spinor), (blank, turned)):
+            term = lax.dot_general(
+                jnp.concatenate([spinor, below], axis=0),
+                right,
+                (((1,), (1,)), ((), ())),
+                preferred_element_type=jnp.float32,
+            )
+            both = term if both is None else both + term
 
     sums = []
-    for grid in (real, imag):
+    for part in range(2):
         for column in range(columns):
             picked = jnp.zeros((1, LANES), jnp.float32)
             for colour in range(COLOURS):
-                row = grid[total + colour : total + colour + 1, column * LANES : (column + 1) * LANES]
+                place = total + 2 * colour + part
+                row = both[place : place + 1, column * LANES : (column + 1) * LANES]
                 picked = jnp.where(colour_of == colour, row, picked)
             sums.append(picked)
     for mask in range(4):
@@ -185,41 +189,27 @@
     wide_high = lax.broadcasted_iota(jnp.int32, (rows, LANES), 1) >= count
     tilt = jnp.where(wide_high, -1.0, 1.0)
     for upper in range(2):
-        blocks = []
-        for pair in range(2):
-            column = upper ^ pair
-            across = slice(column * LANES, (column + 1) * LANES)
-            pieces = []
-            for spin in (2 * pair, 2 * pair + 1):
-                down = slice(spin * count, (spin + 1) * count)
-                r, i = real[down, across], imag[down, across]
-                pieces.append((r + i, r - i))
-            blocks.append(pieces)
         for low in range(2):
-            made = {}
-
-            def part_of(kind, pair, same):
-                if (kind, pair) not in made:
-                    even, odd = blocks[pair][0][kind], blocks[pair][1][kind]
-                    first, second = (odd, even) if low else (even, odd)
-                    kept = jnp.where(wide_high, second[rows:], first[:rows])
-                    moved = half_swap(jnp.where(wide_high, second[:rows], first[rows:]), count)
-                    made[kind, pair] = (kept, moved)
-                kept, moved = made[kind, pair]
-                if (kind, pair, same) not in made:
-                    made[kind, pair, same] = kept + moved if same else tilt * (kept - moved)
-                return made[kind, pair, same]
-
-            for number, (imaginary, anti_one, shift, values) in enumerate(GAMMAS):
-                if shift != low + 2 * upper:
+            made = []
+            for pair in range(2):
+                column = upper ^ pair
+                across = slice(column * LANES, (column + 1) * LANES)
+                spins = (2 * pair + low, 2 * pair + 1 - low)
+                first, second = (both[spin * count : (spin + 1) * count, across] for spin in spins)
+                kept = jnp.where(wide_high, second[rows:], first[:rows])
+                moved = half_swap(jnp.where(wide_high, second[:rows], first[rows:]), count)
+                made.append((tilt * (kept - moved), kept + moved))
+            shift = low + 2 * upper
+            for number, (imaginary, anti_one, mask, values) in enumerate(GAMMAS):
+                if mask != shift:
                     continue
-                kind = imaginary ^ anti_one
+                flip = shift if imaginary ^ anti_one else 0
                 turn = -1 if anti_one and not imaginary else 1
+                signs = [turn * values[spin ^ flip] for spin in range(SPINS)]
                 terms = []
                 for pair in range(2):
-                    first = turn * values[2 * pair + low]
-                    second = turn * values[2 * pair + 1 - low]
-                    terms.append((first, part_of(kind, pair, first == second)))
+                    lead, other = signs[2 * pair + low], signs[2 * pair + 1 - low]
+                    terms.append((lead, made[pair][lead == other]))
                 (one, left), (two, right) = terms
                 if one > 0:
                     value = left + right if two > 0 else left - right
@@ -245,6 +235,8 @@
     rows = count // 2
     own = lax.axis_index("tm")
     anti = notes_ref[pl.ds(0, 1), :] > 0.5
+    scale = 0.5 * gram_scale
+    imag_scale = jnp.where(notes_ref[pl.ds(1, 1), :] > 0.5, -scale, scale)
     high = lax.broadcasted_iota(jnp.int32, (rows, LANES), 1) >= count
     full_high = lax.broadcasted_iota(jnp.int32, (count, LANES), 1) >= count
     for place, (ref, slice_index) in enumerate(((mine_ref, own), (other_ref, 1 - own))):
@@ -254,12 +246,12 @@
             [jnp.where(high, swapped, packed), jnp.where(high, packed, swapped)], axis=0
         )
         turned = jnp.transpose(jnp.concatenate([square, square], axis=0))[:count]
-        real = (square + turned) * (0.5 * gram_scale)
-        imag = (square - turned) * (0.5 * gram_scale)
+        real = (square + turned) * scale
+        imag = (square - turned) * imag_scale
         plain = jnp.where(full_high, imag, real)
         rotated = jnp.where(full_high, real, -imag)
         gram_ref[slice_index] = jnp.where(anti, rotated, plain)
-        row = ref[pl.ds(rows, 1), :] * notes_ref[pl.ds(1 + place, 1), :]
+        row = ref[pl.ds(rows, 1), :] * notes_ref[pl.ds(2 + place, 1), :]
         both = jnp.concatenate([row, half_swap(row, count)], axis=0)
         loop_ref[slice_index] = both[:, :count]
 

time: 18.9 us -> 18.9 us (level)
  no operation moved by 1% of the time
where the time goes in v5:
time: 18.9 us; the launch traced here: 18.8 us
  blocking collectives  14.4 us (76%)
  Pallas kernels  2.43 us (13%)
  waiting for transfers between devices  1.09 us (6%)
  between operations  0.64 us (3%)
    all_to_all x1, blocking collectives, packed_shards(): lax.all_to_all(parts.reshape(owners, chunk, 1, LANES), ('space', 'tm'), 0...  14.4 us
    pallas_call x1, Pallas kernels, packed_shards(): pl.pallas_call(partial(partial_kernel, count, orders, loop_scale), out_sh...  1.62 us
    ppermute x1, waiting for transfers between devices, packed_shards(): other = lax.ppermute(mine, 'tm', [(0, 1), (1, 0)])  1.09 us
    pallas_call x1, Pallas kernels, packed_shards(): pl.pallas_call(partial(finish_kernel, count, gram_scale), out_shape=(jax....  0.79 us
  transfers between devices with their start and end apart: 1, of which 1 were waited for; matrix products, arithmetic and copies ran while one was open for 0% of the time, Pallas kernels for 0%

profile of v5, /device:TPU:0, one launch (start us, length us, event | category | flops | bytes accessed | tf_op | source)
XLA Modules:
  0.0 18.8 jit_solution(1439346297750053552)
XLA Ops:
  0.6 1.6 %partial_gram.1 = (f32[528,128]{1,0:T(8,128)S(1)}, f32[8,128]{1,0:T(8,128)S(1)}) custom-call(s32[16]{0:T(128)} %ids_hbm.1, s32[1,64]{1,0:T(1,128)} %bitcast.10, bf16[1536,128]{1,0:T(8,128)(2,1)} %bitcast.9), custom_call_target="tpu_custom_call" | custom-call | tf_op jit(solution)/shard_map/partial_gram/pallas_call | solution.py:273
  2.3 14.4 %all_to_all.5 = f32[16,33,1,128]{3,2,1,0:T(1,128)S(1)} all-to-all(f32[16,33,1,128]{3,2,1,0:T(1,128)S(1)} %bitcast.8), channel_id=1, replica_groups={{26,16,28,22,10,12,30,8,18,0,4,2,24,20,14,6},{23,19,25,3,5,31,27,13,1,2..., dimensions={0} | all-to-all | bytes 540672 | tf_op jit(solution)/shard_map/all_to_all | solution.py:293
  16.7 0.2 collective-permute-start
  16.9 1.1 %collective-permute-done.other_ref = f32[33,128]{1,0:T(8,128)S(1)} collective-permute-done((f32[33,128]{1,0:T(8,128)S(1)}, f32[33,128]{1,0:T(8,128)S(1)}, u32[]{:S(2)}, u32[]{:S(2)}) %collective-permute-start) | collective-permute-done | bytes 16928 | tf_op jit(solution)/shard_map/ppermute | solution.py:309
  18.0 0.8 %finish.1 = (f32[2,64,128]{2,1,0:T(8,128)}, f32[2,2,64]{2,1,0:T(2,128)}) custom-call(f32[8,128]{1,0:T(8,128)S(1)} %get-tuple-element.6.notes_ref, f32[33,128]{1,0:T(8,128)S(1)} %sum_chunks.1.mine_ref, f32[33,128]{1,0:T(8,128)S(1)} %collective-permute-done.other_ref), custom_call_target="tpu_custom_call" | custom-call | tf_op jit(solution)/shard_map/finish/pallas_call | solution.py:310
  (1 shorter events, 0.0 us)
Async XLA Ops:
  16.7 1.3 %collective-permute-start = (f32[33,128]{1,0:T(8,128)S(1)}, f32[33,128]{1,0:T(8,128)S(1)}, u32[]{:S(2)}, u32[]{:S(2)}) collective-permute-start(f32[33,128]{1,0:T(8,128)S(1)} %sum_chunks.1.mine_ref), channel_id=1, source_target_pairs={{0,1},{1,0},{2,3},{3,2},{4,5},{5,4},{6,7},{7,6},{8,9},{9,8},{10,11... | collective-permute-start | bytes 50696 | tf_op jit(solution)/shard_map/ppermute | solution.py:309

commit v6 on v5

--- a/solution.py
+++ b/solution.py
@@ -15,7 +15,7 @@
 
 EXCHANGE_ORDERS = (
     (13, 8, 14, 11, 5, 6, 15, 4, 9, 0, 2, 1, 12, 10, 7, 3),
-    (11, 9, 12, 1, 2, 15, 13, 6, 0, 10, 5, 8, 3, 7, 4, 14),
+    (11, 9, 6, 4, 12, 15, 13, 2, 0, 10, 5, 8, 3, 7, 1, 14),
 )
 
 

time: 18.9 us -> 18.9 us (level)
  no operation moved by 1% of the time
where the time goes in v6:
time: 18.9 us; the launch traced here: 18.8 us
  blocking collectives  14.4 us (76%)
  Pallas kernels  2.43 us (13%)
  waiting for transfers between devices  1.1 us (6%)
  between operations  0.64 us (3%)
    all_to_all x1, blocking collectives, packed_shards(): lax.all_to_all(parts.reshape(owners, chunk, 1, LANES), ('space', 'tm'), 0...  14.4 us
    pallas_call x1, Pallas kernels, packed_shards(): pl.pallas_call(partial(partial_kernel, count, orders, loop_scale), out_sh...  1.62 us
    ppermute x1, waiting for transfers between devices, packed_shards(): other = lax.ppermute(mine, 'tm', [(0, 1), (1, 0)])  1.1 us
    pallas_call x1, Pallas kernels, packed_shards(): pl.pallas_call(partial(finish_kernel, count, gram_scale), out_shape=(jax....  0.79 us
  transfers between devices with their start and end apart: 1, of which 1 were waited for; matrix products, arithmetic and copies ran while one was open for 0% of the time, Pallas kernels for 0%

profile of v6, /device:TPU:0, one launch (start us, length us, event | category | flops | bytes accessed | tf_op | source)
XLA Modules:
  0.0 18.8 jit_solution(12765835094889602044)
XLA Ops:
  0.6 1.6 %partial_gram.1 = (f32[528,128]{1,0:T(8,128)S(1)}, f32[8,128]{1,0:T(8,128)S(1)}) custom-call(s32[16]{0:T(128)} %ids_hbm.1, s32[1,64]{1,0:T(1,128)} %bitcast.10, bf16[1536,128]{1,0:T(8,128)(2,1)} %bitcast.9), custom_call_target="tpu_custom_call" | custom-call | tf_op jit(solution)/shard_map/partial_gram/pallas_call | solution.py:273
  2.3 14.4 %all_to_all.5 = f32[16,33,1,128]{3,2,1,0:T(1,128)S(1)} all-to-all(f32[16,33,1,128]{3,2,1,0:T(1,128)S(1)} %bitcast.8), channel_id=1, replica_groups={{26,16,28,22,10,12,30,8,18,0,4,2,24,20,14,6},{23,19,13,9,25,31,27,5,1,2..., dimensions={0} | all-to-all | bytes 540672 | tf_op jit(solution)/shard_map/all_to_all | solution.py:293
  16.7 0.2 collective-permute-start
  16.9 1.1 %collective-permute-done.other_ref = f32[33,128]{1,0:T(8,128)S(1)} collective-permute-done((f32[33,128]{1,0:T(8,128)S(1)}, f32[33,128]{1,0:T(8,128)S(1)}, u32[]{:S(2)}, u32[]{:S(2)}) %collective-permute-start) | collective-permute-done | bytes 16928 | tf_op jit(solution)/shard_map/ppermute | solution.py:309
  18.0 0.8 %finish.1 = (f32[2,64,128]{2,1,0:T(8,128)}, f32[2,2,64]{2,1,0:T(2,128)}) custom-call(f32[8,128]{1,0:T(8,128)S(1)} %get-tuple-element.6.notes_ref, f32[33,128]{1,0:T(8,128)S(1)} %sum_chunks.1.mine_ref, f32[33,128]{1,0:T(8,128)S(1)} %collective-permute-done.other_ref), custom_call_target="tpu_custom_call" | custom-call | tf_op jit(solution)/shard_map/finish/pallas_call | solution.py:310
  (1 shorter events, 0.0 us)
Async XLA Ops:
  16.7 1.3 %collective-permute-start = (f32[33,128]{1,0:T(8,128)S(1)}, f32[33,128]{1,0:T(8,128)S(1)}, u32[]{:S(2)}, u32[]{:S(2)}) collective-permute-start(f32[33,128]{1,0:T(8,128)S(1)} %sum_chunks.1.mine_ref), channel_id=1, source_target_pairs={{0,1},{1,0},{2,3},{3,2},{4,5},{5,4},{6,7},{7,6},{8,9},{9,8},{10,11... | collective-permute-start | bytes 50696 | tf_op jit(solution)/shard_map/ppermute | solution.py:309
